TPU v7x, 32 devices: a whole 2x2x4 slice. The times are simulated.
32 devices in a mesh: mp: 4 (over y, x), nodes: 8 (over z, core).
Axes of the slice: x: 2, y: 2, z: 4, core: 2. Of those that a mesh axis runs over, the one named last changes fastest.
Arguments:
- grid_latent: float32 [16384, 512], P('nodes'), may hold values from -6 to 6
- mesh_latent: float32 [1024, 512], P('nodes'), may hold values from -250 to 250
- enc_grid_w: float32 [512, 512], P(None, 'mp'), may hold values from -0.25 to 0.25
- enc_mesh_w: float32 [512, 512], P(None, 'mp'), may hold values from -0.25 to 0.25
- enc_out_w: float32 [512, 512], P('mp'), may hold values from -0.25 to 0.25
- block_gain: float32 [512], replicated, may hold values from 0.5 to 1.5
- query_w: float32 [512, 512], P(None, 'mp'), may hold values from -1 to 1
- key_w: float32 [512, 512], P(None, 'mp'), may hold values from -1 to 1
- value_w: float32 [512, 512], P(None, 'mp'), may hold values from -0.25 to 0.25
- out_w: float32 [512, 512], P('mp'), may hold values from -0.25 to 0.25
- up_w: float32 [512, 2048], P(None, 'mp'), may hold values from -0.25 to 0.25
- down_w: float32 [2048, 512], P('mp'), may hold values from -0.125 to 0.125
- dec_gain: float32 [512], replicated, may hold values from 0.5 to 1.5
- dec_grid_w: float32 [512, 512], P(None, 'mp'), may hold values from -0.25 to 0.25
- dec_mesh_w: float32 [512, 512], P(None, 'mp'), may hold values from -0.25 to 0.25
- dec_out_w: float32 [512, 512], P('mp'), may hold values from -0.25 to 0.25
- neighbor_blocks: int32 [8, 16], replicated, may hold values from 0 to 7, as said below
- enc_tiles: int32 [256, 2], P('nodes'), may hold values from -1 to 127, as said below
- enc_edges: int32 [256, 2, 128], P('nodes'), may hold values from 0 to 127
- dec_tiles: int32 [384, 2], P('nodes'), may hold values from 0 to 127, as said below
- dec_edges: int32 [384, 2, 128], P('nodes'), may hold values from 0 to 127
Outputs:
- grid_out: float32 [16384, 512], P('nodes', 'mp')
Inputs may be any that keep to these rules, and one draw needn't show every extreme that they name: `neighbor_blocks`: rows i * 1 to (i + 1) - 1 are the query blocks of index i of nodes; among all entries of those rows, the blocks of any one index j of nodes (ids j * 1 to (j + 1) - 1) are named at most 4 times, and for every i some j is named exactly 4 times. Entries may repeat. `enc_tiles`: tile slots i * 32 to (i + 1) * 32 - 1 belong to index i of nodes; a live tile names a grid block and a mesh block both of index i; an unused slot holds -1 in both columns; on each index the live slots come first, their number differs between indices, and some index has all 32 slots live. `dec_tiles`: tiles i * 48 to (i + 1) * 48 - 1 belong to index i of nodes; each names a grid block of index i and a mesh block of index i - 1, i or i + 1 of nodes (counted around the axis).
All inputs are finite; a program needn't handle non-finite values.
Results may differ from a plain program's by a relative error of at most 0.000098.
Values sent between devices are 32-bit elements; how exact they have to be, the bound alone decides.
No kernel may reach another device: no remote copies, remote signals or barrier semaphores. Data moves between devices by JAX's collectives and lax.ppermute only.
A program may use at most 128 MiB of HBM per device.

v0:
```python
import math
import jax
import jax.numpy as jnp
from jax import lax
from jax.sharding import PartitionSpec as P

HEAD_DIM = 128
NODE_BLOCK = 128
FULL_PRECISION = lax.Precision.HIGHEST


def padded(shard, sides, width):
    for axis, dim in sides:
        devices, length = (lax.axis_size(axis), shard.shape[dim])
        up = [(i, (i + 1) % devices) for i in range(devices)]
        down = [(j, i) for i, j in up]
        last = lax.slice_in_dim(shard, length - width, length, axis=dim)
        initial = lax.slice_in_dim(shard, 0, width, axis=dim)
        before = lax.ppermute(last, axis, up)
        after = lax.ppermute(initial, axis, down)
        shard = jnp.concatenate([before, shard, after], axis=dim)
    return shard


def product(matrix, weight):
    return jnp.dot(matrix, weight, precision=FULL_PRECISION, preferred_element_type=jnp.float32)


def layer_norm(inputs, scales):
    centre = jnp.mean(inputs, axis=-1, keepdims=True)
    shifted = inputs - centre
    spread = jnp.mean(shifted * shifted, axis=-1, keepdims=True)
    return shifted * lax.rsqrt(spread + 1e-05) * scales


def edge_pass(
    source_side, target_side, source_block, target_block, edge_ids, tile_live, target_blocks
):
    source = source_block[:, None] * NODE_BLOCK + edge_ids[:, 0, :]
    target = target_block[:, None] * NODE_BLOCK + edge_ids[:, 1, :]
    message = jax.nn.silu(source_side[source] + target_side[target]) * tile_live[:, None, None]
    within = (edge_ids[:, 1, :][:, None, :] == jnp.arange(NODE_BLOCK)[None, :, None]).astype(
        jnp.float32
    )
    tile_sums = jnp.einsum("tne,teh->tnh", within, message, precision=FULL_PRECISION)
    placing = (target_block[None, :] == jnp.arange(target_blocks)[:, None]).astype(jnp.float32)
    summed = jnp.einsum("bt,tnh->bnh", placing, tile_sums, precision=FULL_PRECISION)
    return summed.reshape(target_blocks * NODE_BLOCK, -1)


def per_device(
    grid_latent,
    mesh_latent,
    enc_grid_w,
    enc_mesh_w,
    enc_out_w,
    block_gain,
    query_w,
    key_w,
    value_w,
    out_w,
    up_w,
    down_w,
    dec_gain,
    dec_grid_w,
    dec_mesh_w,
    dec_out_w,
    neighbor_blocks,
    enc_tiles,
    enc_edges,
    dec_tiles,
    dec_edges,
):
    me_node = lax.axis_index("nodes")
    nodes_count = lax.axis_size("nodes")
    grid_rows = grid_latent.shape[0]
    node_rows = mesh_latent.shape[0]
    grid_blocks = grid_rows // NODE_BLOCK
    node_blocks = node_rows // NODE_BLOCK
    grid_enc = product(grid_latent, enc_grid_w)
    mesh_enc = product(mesh_latent, enc_mesh_w)
    tile_live = enc_tiles[:, 0] >= 0
    source_block = jnp.where(tile_live, enc_tiles[:, 0] - me_node * grid_blocks, 0)
    target_block = jnp.where(tile_live, enc_tiles[:, 1] - me_node * node_blocks, 0)
    enc_agg = edge_pass(
        grid_enc,
        mesh_enc,
        source_block,
        target_block,
        enc_edges,
        tile_live.astype(jnp.float32),
        node_blocks,
    )
    enc_total = lax.psum(product(enc_agg, enc_out_w), "mp")
    mesh_one = mesh_latent + enc_total
    normed = layer_norm(mesh_one, block_gain)
    queries = product(normed, query_w)
    key_rows = product(normed, key_w)
    value_rows = product(normed, value_w)
    head_cols = queries.shape[1]
    heads_here = head_cols // HEAD_DIM
    key_values = jnp.concatenate([key_rows, value_rows], axis=1)
    query_blocks = queries.reshape(node_blocks, NODE_BLOCK, heads_here, HEAD_DIM)
    own_lists = lax.dynamic_slice_in_dim(neighbor_blocks, me_node * node_blocks, node_blocks, 0)
    key_piece = lax.all_gather(key_values, "nodes", axis=0, tiled=True)
    running_max = jnp.full((node_blocks, heads_here, NODE_BLOCK), -1e30, jnp.float32)
    row_count = key_piece.shape[0]
    piece_block = jnp.arange(row_count) // NODE_BLOCK
    repeats = jnp.sum(
        (own_lists[:, :, None] == piece_block[None, None, :]).astype(jnp.float32), axis=1
    )
    near_keys = key_piece[:, :head_cols].reshape(row_count, heads_here, HEAD_DIM)
    near_values = key_piece[:, head_cols:].reshape(row_count, heads_here, HEAD_DIM)
    scores = jnp.einsum(
        "bqhd,khd->bhqk", query_blocks, near_keys, precision=FULL_PRECISION
    ) / math.sqrt(HEAD_DIM)
    scores = jnp.where((repeats > 0)[:, None, None, :], scores, -1e30)
    new_max = jnp.maximum(running_max, jnp.max(scores, axis=-1))
    weights = jnp.exp(scores - new_max[..., None]) * repeats[:, None, None, :]
    running_sum = jnp.sum(weights, axis=-1)
    running_out = jnp.einsum("bhqk,khd->bhqd", weights, near_values, precision=FULL_PRECISION)
    running_max, running_sum, running_out = (new_max, running_sum, running_out)
    attended = (
        (running_out / running_sum[..., None]).transpose(0, 2, 1, 3).reshape(node_rows, head_cols)
    )
    hidden = jax.nn.silu(product(normed, up_w))
    block_total = lax.psum(product(attended, out_w) + product(hidden, down_w), "mp")
    mesh_two = mesh_one + block_total
    mesh_normed = layer_norm(mesh_two, dec_gain)
    all_blocks = node_blocks * nodes_count
    dec_source = (dec_tiles[:, 0] - (me_node - 1) * node_blocks) % all_blocks
    dec_target = dec_tiles[:, 1] - me_node * grid_blocks
    mesh_dec = product(mesh_normed, dec_mesh_w)
    grid_dec = product(grid_latent, dec_grid_w)
    beside_all = padded(mesh_dec, (("nodes", 0),), node_rows)
    every_tile = jnp.ones((dec_tiles.shape[0],), jnp.float32)
    dec_agg = edge_pass(
        beside_all, grid_dec, dec_source, dec_target, dec_edges, every_tile, grid_blocks
    )
    decoded = lax.psum_scatter(product(dec_agg, dec_out_w), "mp", scatter_dimension=1, tiled=True)
    share_cols = decoded.shape[1]
    grid_share = lax.dynamic_slice_in_dim(
        grid_latent, lax.axis_index("mp") * share_cols, share_cols, 1
    )
    return grid_share + decoded


def solution(mesh):
    in_specs = (
        P("nodes", None),
        P("nodes", None),
        P(None, "mp"),
        P(None, "mp"),
        P("mp", None),
        P(),
        P(None, "mp"),
        P(None, "mp"),
        P(None, "mp"),
        P("mp", None),
        P(None, "mp"),
        P("mp", None),
        P(),
        P(None, "mp"),
        P(None, "mp"),
        P("mp", None),
        P(),
        P("nodes", None),
        P("nodes", None, None),
        P("nodes", None),
        P("nodes", None, None),
    )
    out_specs = P("nodes", "mp")
    return jax.shard_map(
        per_device, mesh=mesh, in_specs=in_specs, out_specs=out_specs, check_vma=False
    )
```

profile of v0, /device:TPU:0, one launch (start us, length us, event | category | flops | bytes accessed | tf_op | source)
XLA Modules:
  0.0 294.3 jit_solution(3935935170186829278)
XLA Ops:
  6.5 0.8 convert_bitcast_fusion
  7.3 0.8 multiply_bitcast_fusion.1
  8.1 0.9 fusion.77
  8.9 1.4 fusion.81
  10.4 5.2 %fusion.80 = f32[2048,128]{1,0:T(8,128)S(1)} fusion(f32[2048,512]{1,0:T(8,128)} %param.21, f32[512,128]{1,0:T(8,128)} %param.23), kind=kOutput, calls=%fused_computation.122 | convolution fusion | flops 1610612736 | bytes 5505024 | tf_op jit(solution)/shard_map/dot_general | solution.py:26
  15.6 0.1 fusion.51
  15.7 14.2 %gather_fusion = f32[4096,128]{1,0:T(8,128)} fusion(f32[2048,128]{1,0:T(8,128)S(1)} %fusion.80, s32[4096]{0:T(1024)S(1)} %get-tuple-element.20), kind=kCustom, calls=%fused_computation | custom fusion | bytes 4210688 | tf_op jit(solution)/shard_map/gather | solution.py:41
  29.9 14.2 %gather_fusion.1 = f32[4096,128]{1,0:T(8,128)} fusion(f32[128,128]{1,0:T(8,128)S(1)} %fusion.81, s32[4096]{0:T(1024)S(1)} %get-tuple-element.21), kind=kCustom, calls=%fused_computation.1 | custom fusion | bytes 4210688 | tf_op jit(solution)/shard_map/gather | solution.py:41
  44.0 1.8 add.225
  45.8 0.0 copy-start.14
  45.9 0.0 copy-start.4
  45.9 1.9 fusion.10
  47.8 0.0 copy-start.3
  47.8 0.0 copy-start.5
  47.8 0.0 copy-start.13
  47.8 0.0 copy-start.6
  47.8 0.0 copy-start.10
  47.9 2.0 fusion.8
  49.8 1.1 fusion.82
  50.9 0.0 all-reduce.3.cloned.1.call-update
  50.9 0.0 all-gather.2.cloned.1.call-start
  51.0 45.9 %all-reduce.3.cloned.1.call-done = f32[128,512]{1,0:T(8,128)} async-done(((f32[128,512]{1,0:T(8,128)}), f32[128,512]{1,0:T(8,128)}) %all-reduce.3.cloned.1.call-update) | async-done | bytes 262160 | tf_op jit(solution)/shard_map/psum | solution.py:94
  96.9 1.1 fusion.75
  97.9 0.2 multiply_reduce_fusion.1
  98.1 0.7 fusion.72
  98.8 0.0 copy-start.7
  98.8 0.7 fusion.73
  99.5 0.7 pad_maximum_fusion.1
  100.1 0.0 all-gather.2.cloned.1.call-update
  100.2 0.2 all-reduce.5.cloned.1.call-start
  100.4 0.7 dynamic-slice_bitcast_fusion
  101.1 0.1 convert_reduce_fusion
  101.2 0.0 copy-start.2
  101.2 5.3 %fusion.83 = f32[2048,128]{1,0:T(8,128)S(1)} fusion(f32[2048,512]{1,0:T(8,128)} %param.21, f32[512,128]{1,0:T(8,128)S(1)} %copy-done.10), kind=kOutput, calls=%fused_computation.125 | convolution fusion | flops 1610612736 | bytes 5505024 | tf_op jit(solution)/shard_map/dot_general | solution.py:26
  106.5 0.0 copy-start.8
  106.5 0.4 fusion.71
  107.0 0.0 copy-start.16
  107.0 0.7 fusion.70
  107.8 0.0 copy-start.15
  107.8 0.7 fusion.34
  108.6 15.6 %all-gather.2.cloned.1.call-done = f32[1024,256]{0,1:T(8,128)} async-done(((f32[128,256]{0,1:T(8,128)}), f32[1024,256]{0,1:T(8,128)}) %all-gather.2.cloned.1.call-update) | async-done | bytes 1048592 | tf_op jit(solution)/shard_map/all_gather | solution.py:105
  124.2 2.1 fusion.78
  126.3 0.2 fusion.29
  126.5 1.8 fusion.22
  128.4 1.1 convolution_add_fusion
  129.5 0.0 all-reduce.5.cloned.1.call-update
  129.5 0.0 reduce-scatter.2.cloned.1.call-start
  129.7 41.8 %all-reduce.5.cloned.1.call-done = f32[128,512]{1,0:T(8,128)} async-done(((f32[128,512]{1,0:T(8,128)}), f32[128,512]{1,0:T(8,128)}) %all-reduce.5.cloned.1.call-update) | async-done | bytes 262160 | tf_op jit(solution)/shard_map/psum | solution.py:127
  171.5 1.1 fusion.74
  172.5 0.2 multiply_reduce_fusion
  172.8 0.4 fusion.31
  173.2 2.3 collective-permute-start.1
  175.6 0.1 fusion.47
  175.6 21.1 %gather_fusion.3 = f32[6144,128]{1,0:T(8,128)} fusion(f32[2048,128]{1,0:T(8,128)S(1)} %fusion.83, s32[6144]{0:T(1024)S(1)} %get-tuple-element.23), kind=kCustom, calls=%fused_computation.3 | custom fusion | bytes 6316032 | tf_op jit(solution)/shard_map/gather | solution.py:41
  196.7 21.0 %gather_fusion.2 = f32[6144,128]{1,0:T(8,128)} fusion(f32[384,128]{1,0:T(8,128)S(1)} %pad_maximum_fusion, s32[6144]{0:T(1024)S(1)} %get-tuple-element.22), kind=kCustom, calls=%fused_computation.2 | custom fusion | bytes 6316032 | tf_op jit(solution)/shard_map/gather | solution.py:41
  217.8 3.2 %add.226 = f32[6144,128]{1,0:T(8,128)S(1)} add(f32[6144,128]{1,0:T(8,128)} %gather_fusion.2, f32[6144,128]{1,0:T(8,128)} %gather_fusion.3) | non-fusion elementwise | flops 786432 | bytes 9437184 | tf_op jit(solution)/shard_map/add | solution.py:41
  220.9 3.0 %fusion.2 = f32[48,128,128]{2,1,0:T(8,128)S(1)} fusion(f32[48,128,128]{2,1,0:T(8,128)S(1)} %bitcast.94, s32[48,128]{1,0:T(8,128)S(1)} %bitcast.98), kind=kOutput, calls=%fused_computation.6 | convolution fusion | flops 1211891712 | bytes 6316032 | tf_op jit(solution)/shard_map/tne,teh->tnh/dot_general | solution.py:45
  223.9 0.0 copy-start.11
  223.9 2.9 fusion
  226.8 0.3 copy.30
  227.2 4.9 %fusion.84 = f32[2048,512]{1,0:T(8,128)} fusion(f32[2048,128]{1,0:T(8,128)S(1)} %bitcast.93, f32[128,512]{1,0:T(8,128)S(1)} %copy-done.11), kind=kOutput, calls=%fused_computation.126 | convolution fusion | flops 1610612736 | bytes 5505024 | tf_op jit(solution)/shard_map/dot_general | solution.py:26
  232.1 0.0 reduce-scatter.2.cloned.1.call-update
  232.2 53.0 %reduce-scatter.2.cloned.1.call-done = f32[2048,128]{1,0:T(8,128)} async-done(((f32[2048,512]{1,0:T(8,128)}), f32[2048,128]{1,0:T(8,128)}) %reduce-scatter.2.cloned.1.call-update) | async-done | bytes 1048592 | tf_op jit(solution)/shard_map/reduce_scatter | solution.py:140
  285.1 2.6 dynamic-slice_add_fusion
  (35 shorter events, 0.2 us)
Async XLA Ops:
  6.5 100.5 %copy-start = (f32[512,512]{1,0:T(8,128)S(1)}, f32[512,512]{1,0:T(8,128)}, u32[]{:S(2)}) copy-start(f32[512,512]{1,0:T(8,128)} %param.31) | copy-start | bytes 3145732
  6.5 90.3 %all-reduce.3.cloned.1.call-start = ((), (), s32[]{:S(2)}) async-start(), calls=%async_computation.1 | async-start | bytes 524288 | tf_op jit(solution)/shard_map/psum | solution.py:94
  29.9 14.2 %copy-start.1 = (f32[4096,128]{1,0:T(8,128)S(1)}, f32[4096,128]{1,0:T(8,128)}, u32[]{:S(2)}) copy-start(f32[4096,128]{1,0:T(8,128)} %gather_fusion) | copy-start | bytes 6291460
  45.8 1.9 copy-start.14
  45.9 4.0 %copy-start.4 = (f32[128,512]{1,0:T(8,128)S(1)}, f32[128,512]{1,0:T(8,128)}, u32[]{:S(2)}) copy-start(f32[128,512]{1,0:T(8,128)} %param.25) | copy-start | bytes 786436
  47.8 49.1 %copy-start.3 = (f32[128,512]{1,0:T(8,128)S(1)}, f32[128,512]{1,0:T(8,128)}, u32[]{:S(2)}) copy-start(f32[128,512]{1,0:T(8,128)} %param.22) | copy-start | bytes 786436
  47.8 50.3 %copy-start.5 = (f32[512,128]{1,0:T(8,128)S(1)}, f32[512,128]{1,0:T(8,128)}, u32[]{:S(2)}) copy-start(f32[512,128]{1,0:T(8,128)} %param.29) | copy-start | bytes 786436
  47.8 50.3 %copy-start.13 = (f32[512]{0:T(512)S(1)}, f32[512]{0:T(512)}, u32[]{:S(2)}) copy-start(f32[512]{0:T(512)} %param.26) | copy-start | bytes 6148
  47.8 51.0 %copy-start.6 = (f32[512,128]{1,0:T(8,128)S(1)}, f32[512,128]{1,0:T(8,128)}, u32[]{:S(2)}) copy-start(f32[512,128]{1,0:T(8,128)} %param.28) | copy-start | bytes 786436
  47.8 53.4 %copy-start.10 = (f32[512,128]{1,0:T(8,128)S(1)}, f32[512,128]{1,0:T(8,128)}, u32[]{:S(2)}) copy-start(f32[512,128]{1,0:T(8,128)} %param.34) | copy-start | bytes 786436
  50.9 73.3 %all-gather.2.cloned.1.call-start = ((), (), s32[]{:S(2)}) async-start(), calls=%async_computation.2 | async-start | bytes 1179648 | tf_op jit(solution)/shard_map/all_gather | solution.py:105
  98.8 7.7 %copy-start.7 = (f32[512,128]{1,0:T(8,128)S(1)}, f32[512,128]{1,0:T(8,128)}, u32[]{:S(2)}) copy-start(f32[512,128]{1,0:T(8,128)} %param.27) | copy-start | bytes 786436
  100.2 71.3 %all-reduce.5.cloned.1.call-start = ((), (), s32[]{:S(2)}) async-start(), calls=%async_computation.3 | async-start | bytes 524288 | tf_op jit(solution)/shard_map/psum | solution.py:127
  101.2 6.6 %copy-start.2 = (f32[512,512]{1,0:T(8,128)S(1)}, f32[512,512]{1,0:T(8,128)}, u32[]{:S(2)}) copy-start(f32[512,512]{1,0:T(8,128)} %param.32) | copy-start | bytes 3145732
  106.5 21.8 %copy-start.8 = (f32[128,512]{1,0:T(8,128)S(1)}, f32[128,512]{1,0:T(8,128)}, u32[]{:S(2)}) copy-start(f32[128,512]{1,0:T(8,128)} %param.30) | copy-start | bytes 786436
  107.0 22.6 %copy-start.16 = (s32[48,2]{0,1:T(2,128)S(1)}, s32[48,2]{0,1:T(2,128)}, u32[]{:S(2)}) copy-start(s32[48,2]{0,1:T(2,128)} %param.40) | copy-start | bytes 1156
  107.0 22.6 %copy-start.12 = (s32[48,2,128]{2,1,0:T(2,128)S(1)}, s32[48,2,128]{2,1,0:T(2,128)}, u32[]{:S(2)}) copy-start(s32[48,2,128]{2,1,0:T(2,128)} %param.41) | copy-start | bytes 147460
  107.8 65.0 %copy-start.9 = (f32[512,128]{1,0:T(8,128)S(1)}, f32[512,128]{1,0:T(8,128)}, u32[]{:S(2)}) copy-start(f32[512,128]{1,0:T(8,128)} %param.35) | copy-start | bytes 786436
  107.8 65.0 %copy-start.15 = (f32[512]{0:T(512)S(1)}, f32[512]{0:T(512)}, u32[]{:S(2)}) copy-start(f32[512]{0:T(512)} %param.33) | copy-start | bytes 6148
  129.5 155.6 %reduce-scatter.2.cloned.1.call-start = ((), (), s32[]{:S(2)}) async-start(), calls=%async_computation.4 | async-start | bytes 5242880 | tf_op jit(solution)/shard_map/reduce_scatter | solution.py:140
  173.2 23.5 %collective-permute-start.1 = (f32[128,128]{1,0:T(8,128)S(1)}, f32[128,128]{1,0:T(8,128)S(1)}, u32[]{:S(2)}, u32[]{:S(2)}) collective-permute-start(f32[128,128]{1,0:T(8,128)S(1)} %fusion.31), channel_id=1, source_target_pairs={{1,0},{2,1},{3,2},{4,3},{5,4},{6,5},{7,6},{0,7},{9,8},{10,9},{11,1... | collective-permute-start | bytes 196616 | tf_op jit(solution)/shard_map/ppermute | solution.py:20
  175.6 21.2 %collective-permute-start = (f32[128,128]{1,0:T(8,128)S(1)}, f32[128,128]{1,0:T(8,128)S(1)}, u32[]{:S(2)}, u32[]{:S(2)}) collective-permute-start(f32[128,128]{1,0:T(8,128)S(1)} %fusion.31), channel_id=1, source_target_pairs={{0,1},{1,2},{2,3},{3,4},{4,5},{5,6},{6,7},{7,0},{8,9},{9,10},{10,1... | collective-permute-start | bytes 196616 | tf_op jit(solution)/shard_map/ppermute | solution.py:19
  223.9 3.3 %copy-start.11 = (f32[128,512]{1,0:T(8,128)S(1)}, f32[128,512]{1,0:T(8,128)}, u32[]{:S(2)}) copy-start(f32[128,512]{1,0:T(8,128)} %param.36) | copy-start | bytes 786436
Sparse Core Ops, SparseCore 0:
  51.0 45.7 all-reduce.2
  100.3 23.8 all-gather.1
  129.6 41.7 all-reduce.4
  232.3 52.8 reduce-scatter.1
where the time goes:
time: 295 us; the launch traced here: 294 us
  waiting for transfers between devices  156 us (53%)
  local copies, waits for them, and re-layouts  72.5 us (25%)
  matrix products  36.4 us (12%)
  between operations  13.6 us (5%)
  other arithmetic  12.8 us (4%)
    reduce_scatter x1, waiting for transfers between devices, per_device(): lax.psum_scatter(product(dec_agg, dec_out_w), 'mp', scatter_dimension=1,...  53 us
    psum x1, waiting for transfers between devices, per_device(): enc_total = lax.psum(product(enc_agg, enc_out_w), 'mp')  45.9 us
    psum x1, waiting for transfers between devices, per_device(): lax.psum(product(attended, out_w) + product(hidden, down_w), 'mp')  41.8 us
    gather x2, local copies, waits for them, and re-layouts, edge_pass(): target_side[target]  35.2 us
    gather x2, local copies, waits for them, and re-layouts, edge_pass(): source_side[source] + target_side[target]  35.2 us
    dot_general x12, matrix products, product(): jnp.dot(matrix, weight, precision=FULL_PRECISION, preferred_element_type=...  22.7 us
    all_gather x1, waiting for transfers between devices, per_device(): key_piece = lax.all_gather(key_values, 'nodes', axis=0, tiled=True)  15.6 us
  transfers between devices with their start and end apart: 6, of which 4 were waited for; matrix products, arithmetic and copies ran while one was open for 10% of the time, Pallas kernels for 0%

commit v1 on v0

--- a/solution.py
+++ b/solution.py
@@ -91,7 +91,9 @@
         tile_live.astype(jnp.float32),
         node_blocks,
     )
-    enc_total = lax.psum(product(enc_agg, enc_out_w), "mp")
+    block = product(enc_agg, enc_out_w)
+    parts = lax.all_gather(block, "mp")
+    enc_total = jnp.sum(parts, axis=0)
     mesh_one = mesh_latent + enc_total
     normed = layer_norm(mesh_one, block_gain)
     queries = product(normed, query_w)

time: 295 us -> 279 us (0.946)
  waiting for transfers between devices: 156 us -> 140 us
    psum x1 -> x0, waiting for transfers between devices: 45.9 us -> none  [per_device(): enc_total = lax.psum(product(enc_agg, enc_out_w), 'mp')]
    all_gather x0 -> x1, waiting for transfers between devices: none -> 29.3 us  [per_device(): parts = lax.all_gather(block, 'mp')]
  transfers between devices with their start and end apart: 6 -> 6, of which waited for: 4 -> 4; matrix products, arithmetic and copies ran while one was open for 10% -> 11% of each run, Pallas kernels for 0% -> 0%
where the time goes in v1:
time: 279 us; the launch traced here: 278 us
  waiting for transfers between devices  140 us (50%)
  local copies, waits for them, and re-layouts  72.5 us (26%)
  matrix products  36.4 us (13%)
  between operations  13.6 us (5%)
  other arithmetic  13.2 us (5%)
    reduce_scatter x1, waiting for transfers between devices, per_device(): lax.psum_scatter(product(dec_agg, dec_out_w), 'mp', scatter_dimension=1,...  53 us
    psum x1, waiting for transfers between devices, per_device(): lax.psum(product(attended, out_w) + product(hidden, down_w), 'mp')  41.8 us
    gather x2, local copies, waits for them, and re-layouts, edge_pass(): target_side[target]  35.2 us
    gather x2, local copies, waits for them, and re-layouts, edge_pass(): source_side[source] + target_side[target]  35.2 us
    all_gather x1, waiting for transfers between devices, per_device(): parts = lax.all_gather(block, 'mp')  29.3 us
    dot_general x12, matrix products, product(): jnp.dot(matrix, weight, precision=FULL_PRECISION, preferred_element_type=...  22.7 us
    all_gather x1, waiting for transfers between devices, per_device(): key_piece = lax.all_gather(key_values, 'nodes', axis=0, tiled=True)  15.6 us
  transfers between devices with their start and end apart: 6, of which 4 were waited for; matrix products, arithmetic and copies ran while one was open for 11% of the time, Pallas kernels for 0%

profile of v1, /device:TPU:0, one launch (start us, length us, event | category | flops | bytes accessed | tf_op | source)
XLA Modules:
  0.0 278.1 jit_solution(11596507774854416266)
XLA Ops:
  6.5 0.8 convert_bitcast_fusion
  7.3 0.8 multiply_bitcast_fusion.1
  8.1 0.9 fusion.77
  8.9 1.4 fusion.81
  10.4 5.2 %fusion.80 = f32[2048,128]{1,0:T(8,128)S(1)} fusion(f32[2048,512]{1,0:T(8,128)} %param.21, f32[512,128]{1,0:T(8,128)} %param.23), kind=kOutput, calls=%fused_computation.122 | convolution fusion | flops 1610612736 | bytes 5505024 | tf_op jit(solution)/shard_map/dot_general | solution.py:26
  15.6 0.1 fusion.51
  15.7 14.2 %gather_fusion = f32[4096,128]{1,0:T(8,128)} fusion(f32[2048,128]{1,0:T(8,128)S(1)} %fusion.80, s32[4096]{0:T(1024)S(1)} %get-tuple-element.20), kind=kCustom, calls=%fused_computation | custom fusion | bytes 4210688 | tf_op jit(solution)/shard_map/gather | solution.py:41
  29.9 14.2 %gather_fusion.1 = f32[4096,128]{1,0:T(8,128)} fusion(f32[128,128]{1,0:T(8,128)S(1)} %fusion.81, s32[4096]{0:T(1024)S(1)} %get-tuple-element.21), kind=kCustom, calls=%fused_computation.1 | custom fusion | bytes 4210688 | tf_op jit(solution)/shard_map/gather | solution.py:41
  44.0 1.8 add.223
  45.8 0.0 copy-start.14
  45.9 0.0 copy-start.4
  45.9 1.9 fusion.10
  47.8 0.0 copy-start.3
  47.8 0.0 copy-start.5
  47.8 0.0 copy-start.13
  47.8 0.0 copy-start.6
  47.8 0.0 copy-start.10
  47.9 2.0 fusion.8
  49.8 1.1 fusion.82
  50.9 0.0 all-gather.6.cloned.1.call-update
  50.9 0.0 all-gather.4.cloned.1.call-start
  51.0 29.3 %all-gather.6.cloned.1.call-done = f32[512,512]{1,0:T(8,128)} async-done(((f32[128,512]{1,0:T(8,128)}), f32[512,512]{1,0:T(8,128)}) %all-gather.6.cloned.1.call-update) | async-done | bytes 1048592 | tf_op jit(solution)/shard_map/all_gather | solution.py:95
  80.3 1.3 reduce_sum.63
  81.6 0.1 fusion.75
  81.8 0.2 multiply_reduce_fusion.1
  82.0 0.7 fusion.72
  82.6 0.0 copy-start.7
  82.7 0.7 fusion.73
  83.3 0.7 pad_maximum_fusion.1
  84.0 0.0 all-gather.4.cloned.1.call-update
  84.0 0.2 all-reduce.2.cloned.1.call-start
  84.2 0.7 dynamic-slice_bitcast_fusion
  84.9 0.1 convert_reduce_fusion
  85.0 0.0 copy-start.2
  85.1 5.3 %fusion.83 = f32[2048,128]{1,0:T(8,128)S(1)} fusion(f32[2048,512]{1,0:T(8,128)} %param.21, f32[512,128]{1,0:T(8,128)S(1)} %copy-done.10), kind=kOutput, calls=%fused_computation.125 | convolution fusion | flops 1610612736 | bytes 5505024 | tf_op jit(solution)/shard_map/dot_general | solution.py:26
  90.4 0.0 copy-start.8
  90.4 0.4 fusion.71
  90.9 0.7 fusion.70
  91.6 0.0 copy-start.9
  91.6 0.8 fusion.34
  92.4 15.6 %all-gather.4.cloned.1.call-done = f32[1024,256]{0,1:T(8,128)} async-done(((f32[128,256]{0,1:T(8,128)}), f32[1024,256]{0,1:T(8,128)}) %all-gather.4.cloned.1.call-update) | async-done | bytes 1048592 | tf_op jit(solution)/shard_map/all_gather | solution.py:107
  108.0 2.1 fusion.78
  110.2 0.2 fusion.29
  110.4 1.8 fusion.22
  112.2 1.1 convolution_add_fusion
  113.3 0.0 all-reduce.2.cloned.1.call-update
  113.3 0.0 reduce-scatter.2.cloned.1.call-start
  113.5 41.8 %all-reduce.2.cloned.1.call-done = f32[128,512]{1,0:T(8,128)} async-done(((f32[128,512]{1,0:T(8,128)}), f32[128,512]{1,0:T(8,128)}) %all-reduce.2.cloned.1.call-update) | async-done | bytes 262160 | tf_op jit(solution)/shard_map/psum | solution.py:129
  155.3 1.1 fusion.74
  156.4 0.2 multiply_reduce_fusion
  156.6 0.4 fusion.31
  157.0 2.3 collective-permute-start.1
  159.4 0.1 fusion.47
  159.5 21.1 %gather_fusion.3 = f32[6144,128]{1,0:T(8,128)} fusion(f32[2048,128]{1,0:T(8,128)S(1)} %fusion.83, s32[6144]{0:T(1024)S(1)} %get-tuple-element.23), kind=kCustom, calls=%fused_computation.3 | custom fusion | bytes 6316032 | tf_op jit(solution)/shard_map/gather | solution.py:41
  180.6 21.0 %gather_fusion.2 = f32[6144,128]{1,0:T(8,128)} fusion(f32[384,128]{1,0:T(8,128)S(1)} %pad_maximum_fusion, s32[6144]{0:T(1024)S(1)} %get-tuple-element.22), kind=kCustom, calls=%fused_computation.2 | custom fusion | bytes 6316032 | tf_op jit(solution)/shard_map/gather | solution.py:41
  201.6 3.2 %add.224 = f32[6144,128]{1,0:T(8,128)S(1)} add(f32[6144,128]{1,0:T(8,128)} %gather_fusion.2, f32[6144,128]{1,0:T(8,128)} %gather_fusion.3) | non-fusion elementwise | flops 786432 | bytes 9437184 | tf_op jit(solution)/shard_map/add | solution.py:41
  204.8 3.0 %fusion.2 = f32[48,128,128]{2,1,0:T(8,128)S(1)} fusion(f32[48,128,128]{2,1,0:T(8,128)S(1)} %bitcast.95, s32[48,128]{1,0:T(8,128)S(1)} %bitcast.100), kind=kOutput, calls=%fused_computation.6 | convolution fusion | flops 1211891712 | bytes 6316032 | tf_op jit(solution)/shard_map/tne,teh->tnh/dot_general | solution.py:45
  207.7 0.0 copy-start.11
  207.7 2.9 %fusion = f32[16,128,128]{2,0,1:T(8,128)S(1)} fusion(f32[48,128,128]{2,1,0:T(8,128)S(1)} %fusion.2, s32[48]{0:T(128)S(1)} %get-tuple-element.13), kind=kOutput, calls=%fused_computation.4 | convolution fusion | flops 150995712 | bytes 4194496 | tf_op jit(solution)/shard_map/bt,tnh->bnh/dot_general | solution.py:47
  210.7 0.3 copy.30
  211.0 4.9 %fusion.84 = f32[2048,512]{1,0:T(8,128)} fusion(f32[2048,128]{1,0:T(8,128)S(1)} %bitcast.94, f32[128,512]{1,0:T(8,128)S(1)} %copy-done.11), kind=kOutput, calls=%fused_computation.126 | convolution fusion | flops 1610612736 | bytes 5505024 | tf_op jit(solution)/shard_map/dot_general | solution.py:26
  216.0 0.0 reduce-scatter.2.cloned.1.call-update
  216.0 53.0 %reduce-scatter.2.cloned.1.call-done = f32[2048,128]{1,0:T(8,128)} async-done(((f32[2048,512]{1,0:T(8,128)}), f32[2048,128]{1,0:T(8,128)}) %reduce-scatter.2.cloned.1.call-update) | async-done | bytes 1048592 | tf_op jit(solution)/shard_map/reduce_scatter | solution.py:142
  269.0 2.6 dynamic-slice_add_fusion
  (36 shorter events, 0.2 us)
Async XLA Ops:
  6.5 84.3 %copy-start = (f32[512,512]{1,0:T(8,128)S(1)}, f32[512,512]{1,0:T(8,128)}, u32[]{:S(2)}) copy-start(f32[512,512]{1,0:T(8,128)} %param.31) | copy-start | bytes 3145732
  6.5 73.8 %all-gather.6.cloned.1.call-start = ((), (), s32[]{:S(2)}) async-start(), calls=%async_computation.4 | async-start | bytes 1310720 | tf_op jit(solution)/shard_map/all_gather | solution.py:95
  29.9 14.2 %copy-start.1 = (f32[4096,128]{1,0:T(8,128)S(1)}, f32[4096,128]{1,0:T(8,128)}, u32[]{:S(2)}) copy-start(f32[4096,128]{1,0:T(8,128)} %gather_fusion) | copy-start | bytes 6291460
  45.8 1.9 copy-start.14
  45.9 4.0 %copy-start.4 = (f32[128,512]{1,0:T(8,128)S(1)}, f32[128,512]{1,0:T(8,128)}, u32[]{:S(2)}) copy-start(f32[128,512]{1,0:T(8,128)} %param.25) | copy-start | bytes 786436
  47.8 33.8 %copy-start.3 = (f32[128,512]{1,0:T(8,128)S(1)}, f32[128,512]{1,0:T(8,128)}, u32[]{:S(2)}) copy-start(f32[128,512]{1,0:T(8,128)} %param.22) | copy-start | bytes 786436
  47.8 34.2 %copy-start.5 = (f32[512,128]{1,0:T(8,128)S(1)}, f32[512,128]{1,0:T(8,128)}, u32[]{:S(2)}) copy-start(f32[512,128]{1,0:T(8,128)} %param.29) | copy-start | bytes 786436
  47.8 34.2 %copy-start.13 = (f32[512]{0:T(512)S(1)}, f32[512]{0:T(512)}, u32[]{:S(2)}) copy-start(f32[512]{0:T(512)} %param.26) | copy-start | bytes 6148
  47.8 34.8 %copy-start.6 = (f32[512,128]{1,0:T(8,128)S(1)}, f32[512,128]{1,0:T(8,128)}, u32[]{:S(2)}) copy-start(f32[512,128]{1,0:T(8,128)} %param.28) | copy-start | bytes 786436
  47.8 37.2 %copy-start.10 = (f32[512,128]{1,0:T(8,128)S(1)}, f32[512,128]{1,0:T(8,128)}, u32[]{:S(2)}) copy-start(f32[512,128]{1,0:T(8,128)} %param.34) | copy-start | bytes 786436
  50.9 57.1 %all-gather.4.cloned.1.call-start = ((), (), s32[]{:S(2)}) async-start(), calls=%async_computation.1 | async-start | bytes 1179648 | tf_op jit(solution)/shard_map/all_gather | solution.py:107
  82.6 7.7 %copy-start.7 = (f32[512,128]{1,0:T(8,128)S(1)}, f32[512,128]{1,0:T(8,128)}, u32[]{:S(2)}) copy-start(f32[512,128]{1,0:T(8,128)} %param.27) | copy-start | bytes 786436
  84.0 71.3 %all-reduce.2.cloned.1.call-start = ((), (), s32[]{:S(2)}) async-start(), calls=%async_computation.2 | async-start | bytes 524288 | tf_op jit(solution)/shard_map/psum | solution.py:129
  85.0 6.6 %copy-start.2 = (f32[512,512]{1,0:T(8,128)S(1)}, f32[512,512]{1,0:T(8,128)}, u32[]{:S(2)}) copy-start(f32[512,512]{1,0:T(8,128)} %param.32) | copy-start | bytes 3145732
  90.4 21.8 %copy-start.8 = (f32[128,512]{1,0:T(8,128)S(1)}, f32[128,512]{1,0:T(8,128)}, u32[]{:S(2)}) copy-start(f32[128,512]{1,0:T(8,128)} %param.30) | copy-start | bytes 786436
  90.8 22.6 %copy-start.16 = (s32[48,2]{0,1:T(2,128)S(1)}, s32[48,2]{0,1:T(2,128)}, u32[]{:S(2)}) copy-start(s32[48,2]{0,1:T(2,128)} %param.40) | copy-start | bytes 1156
  90.9 22.6 %copy-start.12 = (s32[48,2,128]{2,1,0:T(2,128)S(1)}, s32[48,2,128]{2,1,0:T(2,128)}, u32[]{:S(2)}) copy-start(s32[48,2,128]{2,1,0:T(2,128)} %param.41) | copy-start | bytes 147460
  91.6 65.0 %copy-start.9 = (f32[512,128]{1,0:T(8,128)S(1)}, f32[512,128]{1,0:T(8,128)}, u32[]{:S(2)}) copy-start(f32[512,128]{1,0:T(8,128)} %param.35) | copy-start | bytes 786436
  91.6 65.0 %copy-start.15 = (f32[512]{0:T(512)S(1)}, f32[512]{0:T(512)}, u32[]{:S(2)}) copy-start(f32[512]{0:T(512)} %param.33) | copy-start | bytes 6148
  113.3 155.6 %reduce-scatter.2.cloned.1.call-start = ((), (), s32[]{:S(2)}) async-start(), calls=%async_computation.3 | async-start | bytes 5242880 | tf_op jit(solution)/shard_map/reduce_scatter | solution.py:142
  157.0 23.5 %collective-permute-start.1 = (f32[128,128]{1,0:T(8,128)S(1)}, f32[128,128]{1,0:T(8,128)S(1)}, u32[]{:S(2)}, u32[]{:S(2)}) collective-permute-start(f32[128,128]{1,0:T(8,128)S(1)} %fusion.31), channel_id=1, source_target_pairs={{1,0},{2,1},{3,2},{4,3},{5,4},{6,5},{7,6},{0,7},{9,8},{10,9},{11,1... | collective-permute-start | bytes 196616 | tf_op jit(solution)/shard_map/ppermute | solution.py:20
  159.4 21.2 %collective-permute-start = (f32[128,128]{1,0:T(8,128)S(1)}, f32[128,128]{1,0:T(8,128)S(1)}, u32[]{:S(2)}, u32[]{:S(2)}) collective-permute-start(f32[128,128]{1,0:T(8,128)S(1)} %fusion.31), channel_id=1, source_target_pairs={{0,1},{1,2},{2,3},{3,4},{4,5},{5,6},{6,7},{7,0},{8,9},{9,10},{10,1... | collective-permute-start | bytes 196616 | tf_op jit(solution)/shard_map/ppermute | solution.py:19
  207.7 3.3 %copy-start.11 = (f32[128,512]{1,0:T(8,128)S(1)}, f32[128,512]{1,0:T(8,128)}, u32[]{:S(2)}) copy-start(f32[128,512]{1,0:T(8,128)} %param.36) | copy-start | bytes 786436
Sparse Core Ops, SparseCore 0:
  51.0 29.2 all-gather.5
  84.1 23.8 all-gather.3
  113.5 41.8 all-reduce.1
  216.1 52.8 reduce-scatter.1
